TPU v7x, 128 devices: a whole 4x4x4 slice. The times are simulated.
128 devices in a mesh: data: 1, spatial: 64 (over z, y, x), model: 2 (over core).
Axes of the slice: x: 4, y: 4, z: 4, core: 2. Of those that a mesh axis runs over, the one named last changes fastest.
Arguments:
- images: bfloat16 [32, 1024, 14, 512], P('data', 'spatial')
- w_conv1: bfloat16 [3, 3, 512, 512], P(None, None, None, 'model')
- b_conv1: float32 [512], P('model')
- w_conv2: bfloat16 [3, 3, 512, 512], P(None, None, 'model')
- b_conv2: float32 [512], replicated
- w_conv3: bfloat16 [3, 3, 512, 512], P(None, None, None, 'model')
- b_conv3: float32 [512], P('model')
Outputs:
- output: bfloat16 [32, 1024, 14, 512], P('data', 'spatial', None, 'model')
All inputs are finite; a program needn't handle non-finite values.
Results may differ from a plain program's by a relative error of at most 0.00182.
Values are sent between devices in bfloat16 or wider.
A program may use at most 1 GiB of HBM per device.

v0:
```python
import jax
import jax.numpy as jnp
from jax import lax
from jax.sharding import PartitionSpec as P


def conv_rows(padded, kernel):
    return lax.conv_general_dilated(padded, kernel, (1, 1), ((0, 0), (1, 1)), dimension_numbers=("NHWC", "HWIO", "NHWC"), preferred_element_type=jnp.float32)


def add_edge_rows(block, axis_name, n_dev):
    if n_dev == 1:
        return jnp.pad(block, ((0, 0), (1, 1), (0, 0), (0, 0)))
    to_next = [(dev_rank, dev_rank + 1) for dev_rank in range(n_dev - 1)]
    to_prev = [(dev_rank + 1, dev_rank) for dev_rank in range(n_dev - 1)]
    row_above = lax.ppermute(block[:, -1:], axis_name, to_next)
    row_below = lax.ppermute(block[:, :1], axis_name, to_prev)
    return jnp.concatenate([row_above, block, row_below], axis=1)


def solution(mesh):
    n_spatial = mesh.shape["spatial"]

    def local_stack(images, w_conv1, b_conv1, w_conv2, b_conv2, w_conv3, b_conv3):
        act_one = jax.nn.relu(conv_rows(add_edge_rows(images, "spatial", n_spatial), w_conv1) + b_conv1).astype(jnp.bfloat16)
        part_sum = conv_rows(add_edge_rows(act_one, "spatial", n_spatial), w_conv2)
        full_sum = lax.psum(part_sum, "model")
        act_two = jax.nn.relu(full_sum + b_conv2).astype(jnp.bfloat16)
        return jax.nn.relu(conv_rows(add_edge_rows(act_two, "spatial", n_spatial), w_conv3) + b_conv3).astype(jnp.bfloat16)

    in_specs = (
        P("data", "spatial", None, None),
        P(None, None, None, "model"),
        P("model"),
        P(None, None, "model", None),
        P(None),
        P(None, None, None, "model"),
        P("model"),
    )
    return jax.shard_map(local_stack, mesh=mesh, in_specs=in_specs, out_specs=P("data", "spatial", None, "model"), check_vma=False)
```

profile of v0, /device:TPU:30, one launch (start us, length us, event | category | flops | bytes accessed | tf_op | source)
XLA Modules:
  0.0 209.9 jit_solution(8825717401755291834)
XLA Ops:
  6.5 0.0 copy-start
  6.5 0.0 copy-start.4
  6.5 0.0 all-reduce.2.cloned.1.call-start
  6.5 0.0 copy-start.3
  6.5 7.4 %copy.8 = bf16[32,16,14,512]{3,0,2,1:T(8,128)(2,1)S(1)} copy(bf16[32,16,14,512]{3,1,2,0:T(8,128)(2,1)} %param.7) | data formatting | bytes 14680064 | tf_op args[0]
  13.9 0.1 fusion.26
  14.0 3.4 %collective-permute-start = (bf16[32,1,14,512]{3,0,2,1:T(8,128)(2,1)S(1)}, bf16[32,1,14,512]{3,0,2,1:T(8,128)(2,1)S(1)}, u32[]{:S(2)}, u32[]{:S(2)}) collective-permute-start(bf16[32,1,14,512]{3,0,2,1:T(8,128)(2,1)S(1)} %get-tuple-element.7), channel_id=1, source_target_pairs={{0,2},{2,4},{4,6},{6,8},{8,10},{10,12},{12,14},{14,16},{16,18},{18... | collective-permute-start | bytes 1376264 | tf_op jit(solution)/shard_map/ppermute | solution.py:16
  17.4 2.4 %collective-permute-start.1 = (bf16[32,1,14,512]{3,0,2,1:T(8,128)(2,1)S(1)}, bf16[32,1,14,512]{3,0,2,1:T(8,128)(2,1)S(1)}, u32[]{:S(2)}, u32[]{:S(2)}) collective-permute-start(bf16[32,1,14,512]{3,0,2,1:T(8,128)(2,1)S(1)} %get-tuple-element.8), channel_id=1, source_target_pairs={{2,0},{4,2},{6,4},{8,6},{10,8},{12,10},{14,12},{16,14},{18,16},{20... | collective-permute-start | bytes 1376264 | tf_op jit(solution)/shard_map/ppermute | solution.py:17
  19.9 8.3 %collective-permute-done = bf16[32,1,14,512]{3,0,2,1:T(8,128)(2,1)S(1)} collective-permute-done((bf16[32,1,14,512]{3,0,2,1:T(8,128)(2,1)S(1)}, bf16[32,1,14,512]{3,0,2,1:T(8,128)(2,1)S(1)}, u32[]{:S(2)}, u32[]{:S(2)}) %collective-permute-start) | collective-permute-done | bytes 458784 | tf_op jit(solution)/shard_map/ppermute | solution.py:16
  28.2 7.9 %collective-permute-done.1 = bf16[32,1,14,512]{3,0,2,1:T(8,128)(2,1)S(1)} collective-permute-done((bf16[32,1,14,512]{3,0,2,1:T(8,128)(2,1)S(1)}, bf16[32,1,14,512]{3,0,2,1:T(8,128)(2,1)S(1)}, u32[]{:S(2)}, u32[]{:S(2)}) %collective-permute-start.1) | collective-permute-done | bytes 458784 | tf_op jit(solution)/shard_map/ppermute | solution.py:17
  36.0 0.0 copy-done.4
  36.0 0.0 copy-done.3
  36.0 18.4 %maximum_convert_fusion.2 = bf16[32,16,14,256]{3,0,2,1:T(8,128)(2,1)S(1)} fusion(f32[256]{0:T(256)S(1)} %copy-done.4, bf16[3,3,512,256]{3,2,1,0:T(8,128)(2,1)S(1)} %copy-done.3, bf16[32,1,14,512]{3,0,2,1:T(8,128)(2,1)S(1)} %collective-permute-done.1, bf16[32,16,14,512]{3,0,2,1:T(8,128)(2,1)S(1)} %copy.8, bf16[32,1,14,512]{3,0,2,1:T(8,128)(2,1)S(1)} %collective-permute-done), kind=kOutput, calls=%fused_computation.14 | convolution fusion | flops 16136404992 | bytes 14287872 | tf_op jit(solution)/shard_map/conv_general_dilated | solution.py:8
  54.5 1.9 collective-permute-start.2
  56.4 4.1 %collective-permute-start.3 = (bf16[32,1,14,256]{3,0,2,1:T(8,128)(2,1)S(1)}, bf16[32,1,14,256]{3,0,2,1:T(8,128)(2,1)S(1)}, u32[]{:S(2)}, u32[]{:S(2)}) collective-permute-start(bf16[32,1,14,256]{3,0,2,1:T(8,128)(2,1)S(1)} %get-tuple-element.10), channel_id=1, source_target_pairs={{2,0},{4,2},{6,4},{8,6},{10,8},{12,10},{14,12},{16,14},{18,16},{20... | collective-permute-start | bytes 688136 | tf_op jit(solution)/shard_map/ppermute | solution.py:17
  60.5 1.9 collective-permute-done.2
  62.4 6.1 %collective-permute-done.3 = bf16[32,1,14,256]{3,0,2,1:T(8,128)(2,1)S(1)} collective-permute-done((bf16[32,1,14,256]{3,0,2,1:T(8,128)(2,1)S(1)}, bf16[32,1,14,256]{3,0,2,1:T(8,128)(2,1)S(1)}, u32[]{:S(2)}, u32[]{:S(2)}) %collective-permute-start.3) | collective-permute-done | bytes 229408 | tf_op jit(solution)/shard_map/ppermute | solution.py:17
  68.5 0.0 copy-done
  68.5 21.0 %fusion.12 = f32[32,16,14,512]{3,0,2,1:T(8,128)} fusion(bf16[3,3,256,512]{3,2,1,0:T(8,128)(2,1)S(1)} %copy-done, bf16[32,1,14,256]{3,0,2,1:T(8,128)(2,1)S(1)} %collective-permute-done.3, bf16[32,16,14,256]{3,0,2,1:T(8,128)(2,1)S(1)} %maximum_convert_fusion.2, bf16[32,1,14,256]{3,0,2,1:T(8,128)(2,1)S(1)} %collective-permute-done.2), kind=kOutput, calls=%fused_computation.15 | convolution fusion | flops 16118513664 | bytes 21168128 | tf_op jit(solution)/shard_map/conv_general_dilated | solution.py:8
  89.5 0.0 copy-start.2
  89.5 0.0 all-reduce.2.cloned.1.call-update
  89.6 0.0 copy-start.5
  89.6 54.6 %all-reduce.2.cloned.1.call-done = f32[32,16,14,512]{3,0,2,1:T(8,128)} async-done(((f32[32,16,14,512]{3,0,2,1:T(8,128)}), f32[32,16,14,512]{3,0,2,1:T(8,128)}) %all-reduce.2.cloned.1.call-update) | async-done | bytes 14680080 | tf_op jit(solution)/shard_map/psum | solution.py:27
  144.2 0.0 copy-done.2
  144.2 10.4 %maximum_convert_fusion = bf16[32,16,14,512]{3,0,2,1:T(8,128)(2,1)} fusion(f32[32,16,14,512]{3,0,2,1:T(8,128)} %all-reduce.2.cloned.1.call-done, f32[512]{0:T(512)S(1)} %copy-done.2), kind=kLoop, calls=%fused_computation | loop fusion | flops 11010048 | bytes 22022144 | tf_op jit(solution)/shard_map/convert_element_type | solution.py:28
  154.6 1.2 fusion.25
  155.9 3.4 %collective-permute-start.4 = (bf16[32,1,14,512]{3,0,2,1:T(8,128)(2,1)S(1)}, bf16[32,1,14,512]{3,0,2,1:T(8,128)(2,1)S(1)}, u32[]{:S(2)}, u32[]{:S(2)}) collective-permute-start(bf16[32,1,14,512]{3,0,2,1:T(8,128)(2,1)S(1)} %get-tuple-element.5), channel_id=1, source_target_pairs={{0,2},{2,4},{4,6},{6,8},{8,10},{10,12},{12,14},{14,16},{16,18},{18... | collective-permute-start | bytes 1376264 | tf_op jit(solution)/shard_map/ppermute | solution.py:16
  159.3 2.7 %collective-permute-start.5 = (bf16[32,1,14,512]{3,0,2,1:T(8,128)(2,1)S(1)}, bf16[32,1,14,512]{3,0,2,1:T(8,128)(2,1)S(1)}, u32[]{:S(2)}, u32[]{:S(2)}) collective-permute-start(bf16[32,1,14,512]{3,0,2,1:T(8,128)(2,1)S(1)} %get-tuple-element.6), channel_id=1, source_target_pairs={{2,0},{4,2},{6,4},{8,6},{10,8},{12,10},{14,12},{16,14},{18,16},{20... | collective-permute-start | bytes 1376264 | tf_op jit(solution)/shard_map/ppermute | solution.py:17
  162.0 8.5 %collective-permute-done.4 = bf16[32,1,14,512]{3,0,2,1:T(8,128)(2,1)S(1)} collective-permute-done((bf16[32,1,14,512]{3,0,2,1:T(8,128)(2,1)S(1)}, bf16[32,1,14,512]{3,0,2,1:T(8,128)(2,1)S(1)}, u32[]{:S(2)}, u32[]{:S(2)}) %collective-permute-start.4) | collective-permute-done | bytes 458784 | tf_op jit(solution)/shard_map/ppermute | solution.py:16
  170.5 7.8 %collective-permute-done.5 = bf16[32,1,14,512]{3,0,2,1:T(8,128)(2,1)S(1)} collective-permute-done((bf16[32,1,14,512]{3,0,2,1:T(8,128)(2,1)S(1)}, bf16[32,1,14,512]{3,0,2,1:T(8,128)(2,1)S(1)}, u32[]{:S(2)}, u32[]{:S(2)}) %collective-permute-start.5) | collective-permute-done | bytes 458784 | tf_op jit(solution)/shard_map/ppermute | solution.py:17
  178.3 0.0 copy-done.5
  178.3 0.0 copy-start.1
  178.3 20.8 %maximum_convert_fusion.1 = bf16[32,16,14,256]{3,0,2,1:T(8,128)(2,1)S(1)} fusion(f32[256]{0:T(256)S(1)} %copy-done.5, bf16[3,3,512,256]{3,2,1,0:T(8,128)(2,1)} %param.12, bf16[32,1,14,512]{3,0,2,1:T(8,128)(2,1)S(1)} %collective-permute-done.5, bf16[32,16,14,512]{3,0,2,1:T(8,128)(2,1)} %maximum_convert_fusion, ...), kind=kOutput, calls=%fused_computation.13 | convolution fusion | flops 16136404992 | bytes 14287872 | tf_op jit(solution)/shard_map/conv_general_dilated | solution.py:8
  199.1 4.0 %copy.11 = bf16[32,16,14,256]{3,1,2,0:T(8,128)(2,1)} copy(bf16[32,16,14,256]{3,0,2,1:T(8,128)(2,1)S(1)} %maximum_convert_fusion.1) | data formatting | bytes 7340032 | tf_op jit(solution)/shard_map/convert_element_type | solution.py:29
  203.1 0.0 copy-done.1
  (1 shorter events, 0.0 us)
Async XLA Ops:
  6.5 62.0 %copy-start = (bf16[3,3,256,512]{3,2,1,0:T(8,128)(2,1)S(1)}, bf16[3,3,256,512]{3,2,1,0:T(8,128)(2,1)}, u32[]{:S(2)}) copy-start(bf16[3,3,256,512]{3,2,1,0:T(8,128)(2,1)} %param.10) | copy-start | bytes 7077892
  6.5 29.5 %copy-start.4 = (f32[256]{0:T(256)S(1)}, f32[256]{0:T(256)}, u32[]{:S(2)}) copy-start(f32[256]{0:T(256)} %param.9) | copy-start | bytes 3076
  6.5 137.7 %all-reduce.2.cloned.1.call-start = ((), (), s32[]{:S(2)}) async-start(), calls=%async_computation | async-start | bytes 29360128 | tf_op jit(solution)/shard_map/psum | solution.py:27
  6.5 29.5 %copy-start.3 = (bf16[3,3,512,256]{3,2,1,0:T(8,128)(2,1)S(1)}, bf16[3,3,512,256]{3,2,1,0:T(8,128)(2,1)}, u32[]{:S(2)}) copy-start(bf16[3,3,512,256]{3,2,1,0:T(8,128)(2,1)} %param.8) | copy-start | bytes 7077892
  14.0 14.2 %collective-permute-start = (bf16[32,1,14,512]{3,0,2,1:T(8,128)(2,1)S(1)}, bf16[32,1,14,512]{3,0,2,1:T(8,128)(2,1)S(1)}, u32[]{:S(2)}, u32[]{:S(2)}) collective-permute-start(bf16[32,1,14,512]{3,0,2,1:T(8,128)(2,1)S(1)} %get-tuple-element.7), channel_id=1, source_target_pairs={{0,2},{2,4},{4,6},{6,8},{8,10},{10,12},{12,14},{14,16},{16,18},{18... | collective-permute-start | bytes 1376264 | tf_op jit(solution)/shard_map/ppermute | solution.py:16
  17.4 18.6 %collective-permute-start.1 = (bf16[32,1,14,512]{3,0,2,1:T(8,128)(2,1)S(1)}, bf16[32,1,14,512]{3,0,2,1:T(8,128)(2,1)S(1)}, u32[]{:S(2)}, u32[]{:S(2)}) collective-permute-start(bf16[32,1,14,512]{3,0,2,1:T(8,128)(2,1)S(1)} %get-tuple-element.8), channel_id=1, source_target_pairs={{2,0},{4,2},{6,4},{8,6},{10,8},{12,10},{14,12},{16,14},{18,16},{20... | collective-permute-start | bytes 1376264 | tf_op jit(solution)/shard_map/ppermute | solution.py:17
  54.5 7.9 %collective-permute-start.2 = (bf16[32,1,14,256]{3,0,2,1:T(8,128)(2,1)S(1)}, bf16[32,1,14,256]{3,0,2,1:T(8,128)(2,1)S(1)}, u32[]{:S(2)}, u32[]{:S(2)}) collective-permute-start(bf16[32,1,14,256]{3,0,2,1:T(8,128)(2,1)S(1)} %get-tuple-element.9), channel_id=1, source_target_pairs={{0,2},{2,4},{4,6},{6,8},{8,10},{10,12},{12,14},{14,16},{16,18},{18... | collective-permute-start | bytes 688136 | tf_op jit(solution)/shard_map/ppermute | solution.py:16
  56.4 12.1 %collective-permute-start.3 = (bf16[32,1,14,256]{3,0,2,1:T(8,128)(2,1)S(1)}, bf16[32,1,14,256]{3,0,2,1:T(8,128)(2,1)S(1)}, u32[]{:S(2)}, u32[]{:S(2)}) collective-permute-start(bf16[32,1,14,256]{3,0,2,1:T(8,128)(2,1)S(1)} %get-tuple-element.10), channel_id=1, source_target_pairs={{2,0},{4,2},{6,4},{8,6},{10,8},{12,10},{14,12},{16,14},{18,16},{20... | collective-permute-start | bytes 688136 | tf_op jit(solution)/shard_map/ppermute | solution.py:17
  89.5 54.7 %copy-start.2 = (f32[512]{0:T(512)S(1)}, f32[512]{0:T(512)}, u32[]{:S(2)}) copy-start(f32[512]{0:T(512)} %param.11) | copy-start | bytes 6148
  89.6 88.8 %copy-start.5 = (f32[256]{0:T(256)S(1)}, f32[256]{0:T(256)}, u32[]{:S(2)}) copy-start(f32[256]{0:T(256)} %param.13) | copy-start | bytes 3076
  155.9 14.6 %collective-permute-start.4 = (bf16[32,1,14,512]{3,0,2,1:T(8,128)(2,1)S(1)}, bf16[32,1,14,512]{3,0,2,1:T(8,128)(2,1)S(1)}, u32[]{:S(2)}, u32[]{:S(2)}) collective-permute-start(bf16[32,1,14,512]{3,0,2,1:T(8,128)(2,1)S(1)} %get-tuple-element.5), channel_id=1, source_target_pairs={{0,2},{2,4},{4,6},{6,8},{8,10},{10,12},{12,14},{14,16},{16,18},{18... | collective-permute-start | bytes 1376264 | tf_op jit(solution)/shard_map/ppermute | solution.py:16
  159.3 19.0 %collective-permute-start.5 = (bf16[32,1,14,512]{3,0,2,1:T(8,128)(2,1)S(1)}, bf16[32,1,14,512]{3,0,2,1:T(8,128)(2,1)S(1)}, u32[]{:S(2)}, u32[]{:S(2)}) collective-permute-start(bf16[32,1,14,512]{3,0,2,1:T(8,128)(2,1)S(1)} %get-tuple-element.6), channel_id=1, source_target_pairs={{2,0},{4,2},{6,4},{8,6},{10,8},{12,10},{14,12},{16,14},{18,16},{20... | collective-permute-start | bytes 1376264 | tf_op jit(solution)/shard_map/ppermute | solution.py:17
  178.3 24.7 %copy-start.1 = (bf16[3,3,256,512]{3,2,1,0:T(8,128)(2,1)S(1)}, bf16[3,3,256,512]{3,2,1,0:T(8,128)(2,1)}, u32[]{:S(2)}) copy-start(bf16[3,3,256,512]{3,2,1,0:T(8,128)(2,1)} %param.10) | copy-start | bytes 7077892
Sparse Core Ops, SparseCore 0:
  89.7 54.4 all-reduce.1
where the time goes:
time: 210 us
  waiting for transfers between devices  95.2 us (45%)
  matrix products  60.2 us (29%)
  starting transfers between devices  17.9 us (9%)
  between operations  13.5 us (6%)
  local copies, waits for them, and re-layouts  12.7 us (6%)
  other arithmetic  10.4 us (5%)
    conv_general_dilated x3, matrix products, conv_rows(): lax.conv_general_dilated(padded, kernel, (1, 1), ((0, 0), (1, 1)), dimens...  60.2 us
    psum x1, waiting for transfers between devices, local_stack(): full_sum = lax.psum(part_sum, 'model')  54.6 us
    ppermute x3, waiting for transfers between devices, add_edge_rows(): row_below = lax.ppermute(block[:, :1], axis_name, to_prev)  21.8 us
    ppermute x3, waiting for transfers between devices, add_edge_rows(): row_above = lax.ppermute(block[:, -1:], axis_name, to_next)  18.7 us
    convert_element_type x1, other arithmetic, local_stack(): act_two = jax.nn.relu(full_sum + b_conv2).astype(jnp.bfloat16)  10.4 us
    ppermute x3, starting transfers between devices, add_edge_rows(): row_below = lax.ppermute(block[:, :1], axis_name, to_prev)  9.23 us
    ppermute x3, starting transfers between devices, add_edge_rows(): row_above = lax.ppermute(block[:, -1:], axis_name, to_next)  8.7 us
    unnamed x13, local copies, waits for them, and re-layouts  7.4 us
  transfers between devices with their start and end apart: 7, of which 7 were waited for; matrix products, arithmetic and copies ran while one was open for 0% of the time, Pallas kernels for 0%

commit v1 on v0

v1 whole, which is shorter than its diff:
```python
import functools

import jax
import jax.numpy as jnp
from jax import lax
from jax.experimental import pallas as pl
from jax.experimental.pallas import tpu as pltpu
from jax.sharding import PartitionSpec as P

MESH = pl.DeviceIdType.MESH
ROWS = 4


def kernel(
    dims, img, w1, b1, w2, b2, w3, b3, out,
    stage, act, wts, bias_own, bias_far,
    img_sem, w_sem, w_send, w_recv, b_sem, b_send, b_recv, h_send, h_recv, o_sem, o_send, o_recv,
):
    n_band, batch, height, width, ch = dims
    half, per_core = ch // 2, batch // 2
    core = lax.axis_index("model")
    band = lax.axis_index("spatial")
    data = lax.axis_index("data")
    above, below = lax.rem(band + n_band - 1, n_band), lax.rem(band + 1, n_band)
    sibling = (data, band, 1 - core)
    top, bottom = height + 2, height + 3

    to_above = jnp.where(band == 0, bottom, height + 1)
    to_below = jnp.where(band == n_band - 1, top, 0)

    images_in = pltpu.make_async_copy(img.at[pl.ds(core * per_core, per_core)], stage, img_sem)
    images_in.start()
    own_parts = [wts.at[0, :, :, 0:half], wts.at[1, :, 0:half, :], wts.at[2, :, :, 0:half]]
    far_parts = [wts.at[0, :, :, half:ch], wts.at[1, :, half:ch, :], wts.at[2, :, :, half:ch]]
    w_in = [pltpu.make_async_copy(w, own_parts[i], w_sem.at[i]) for i, w in enumerate((w1, w2, w3))]
    b_in = [
        pltpu.make_async_copy(b1, bias_own.at[0], b_sem.at[0]),
        pltpu.make_async_copy(b2.at[:, 0:half], bias_own.at[1], b_sem.at[1]),
        pltpu.make_async_copy(b2.at[:, half:ch], bias_far.at[1], b_sem.at[2]),
        pltpu.make_async_copy(b3, bias_own.at[2], b_sem.at[3]),
    ]
    w_in[0].start()
    for c in b_in:
        c.start()

    zero_row = jnp.zeros((width + 2, per_core, ch), jnp.bfloat16)
    zero_col = jnp.zeros((1, per_core, ch), jnp.bfloat16)

    def zero(level, _):
        act[level, 0] = zero_row
        act[level, height + 1] = zero_row

        def cols(r, _):
            act[level, r, 0:1] = zero_col
            act[level, r, width + 1 : width + 2] = zero_col
            return 0

        lax.fori_loop(1, height + 1, cols, 0)
        return 0

    lax.fori_loop(0, 3, zero, 0)

    barrier = pltpu.get_barrier_semaphore()
    for who in ((data, above, core), (data, below, core), sibling):
        pl.semaphore_signal(barrier, inc=1, device_id=who, device_id_type=MESH)
    pl.semaphore_wait(barrier, 3)

    w_far = [
        pltpu.make_async_remote_copy(w, far_parts[i], w_send.at[i], w_recv.at[i], device_id=sibling, device_id_type=MESH)
        for i, w in enumerate((w1, w2, w3))
    ]
    b_far = [
        pltpu.make_async_remote_copy(b, bias_far.at[i], b_send.at[k], b_recv.at[k], device_id=sibling, device_id_type=MESH)
        for k, (b, i) in enumerate(((b1, 0), (b3, 2)))
    ]
    w_far[0].start()
    for c in b_far:
        c.start()

    def halo_up(level):
        return pltpu.make_async_remote_copy(
            act.at[level, 1, 1 : width + 1], act.at[level, to_above, 1 : width + 1],
            h_send.at[level, 0], h_recv.at[level, 0], device_id=(data, above, core), device_id_type=MESH,
        )

    def halo_down(level):
        return pltpu.make_async_remote_copy(
            act.at[level, height, 1 : width + 1], act.at[level, to_below, 1 : width + 1],
            h_send.at[level, 1], h_recv.at[level, 1], device_id=(data, below, core), device_id_type=MESH,
        )

    def send_halo(level):
        halo_up(level).start()
        halo_down(level).start()

    def wait_halo(level):
        halo_up(level).wait_recv()
        halo_down(level).wait_recv()

    def take(col, _):
        act[0, 1 : height + 1, col + 1] = jnp.swapaxes(stage[:, col], 0, 1)
        return 0

    images_in.wait()
    lax.fori_loop(0, width, take, 0)
    send_halo(0)
    w_in[1].start()
    w_in[2].start()
    w_far[1].start()
    w_far[2].start()
    for c in b_in:
        c.wait()
    for c in b_far:
        c.wait_recv()

    def conv(level, rows):
        m = width * per_core
        taps = []
        for dh in range(3):
            for dw in range(3):
                views = [act[level, r + dh, dw : dw + width].reshape(m, ch) for r in rows]
                taps.append(jnp.concatenate(views, axis=0))
        lhs = jnp.concatenate(taps, axis=1)
        total = jnp.dot(lhs, wts[level].reshape(9 * ch, ch), preferred_element_type=jnp.float32)
        bias = jnp.concatenate([bias_own[level], bias_far[level]], axis=1)
        return jnp.maximum(total + bias, 0.0).astype(jnp.bfloat16).reshape(ROWS, width, per_core, ch)

    n_chunk = height // ROWS

    def rows_of(j):
        return [lax.rem(1 + ROWS * j + i, height) for i in range(ROWS)]

    def layer(level):
        w_in[level].wait()
        w_far[level].wait_recv()

        def chunk(j, _):
            @pl.when(j == n_chunk - 1)
            def _():
                wait_halo(level)

            rows = rows_of(j)
            y = conv(level, rows)
            for i, r in enumerate(rows):
                act[(level + 1) % 3, r + 1, 1 : width + 1] = y[i]
            return 0

        lax.fori_loop(0, n_chunk, chunk, 0)

    layer(0)
    send_halo(1)
    layer(1)
    send_halo(2)
    halo_up(0).wait_send()
    halo_down(0).wait_send()
    layer(2)

    mine = pl.ds(core * per_core, per_core)

    def own_out(col):
        return pltpu.make_async_copy(stage.at[:, col, :, 0:half], out.at[mine, col], o_sem.at[col])

    def far_out(col):
        return pltpu.make_async_remote_copy(
            stage.at[:, col, :, half:ch], out.at[mine, col], o_send.at[col], o_recv.at[col],
            device_id=sibling, device_id_type=MESH,
        )

    def give(col, _):
        stage[:, col] = jnp.swapaxes(act[0, 1 : height + 1, col + 1], 0, 1)
        far_out(col).start()
        own_out(col).start()
        return 0

    lax.fori_loop(0, width, give, 0)

    for i in range(3):
        w_far[i].wait_send()
    for level in (1, 2):
        halo_up(level).wait_send()
        halo_down(level).wait_send()
    for c in b_far:
        c.wait_send()

    def finish(col, _):
        own_out(col).wait()
        far_out(col).wait_send()
        far_out(col).wait_recv()
        return 0

    lax.fori_loop(0, width, finish, 0)


def solution(mesh):
    n_band = mesh.shape["spatial"]

    def local_stack(images, w_conv1, b_conv1, w_conv2, b_conv2, w_conv3, b_conv3):
        batch, height, width, ch = images.shape
        half, per_core = ch // 2, batch // 2
        hbm = pl.BlockSpec(memory_space=pltpu.HBM)
        dma = pltpu.SemaphoreType.DMA
        flops = 2 * 3 * 9 * per_core * height * width * ch * ch
        y = pl.pallas_call(
            functools.partial(kernel, (n_band, batch, height, width, ch)),
            out_shape=jax.ShapeDtypeStruct((batch, width, height, half), jnp.bfloat16),
            in_specs=[hbm] * 7,
            out_specs=hbm,
            scratch_shapes=[
                pltpu.VMEM((per_core, width, height, ch), jnp.bfloat16),
                pltpu.VMEM((3, height + 4, width + 2, per_core, ch), jnp.bfloat16),
                pltpu.VMEM((3, 9, ch, ch), jnp.bfloat16),
                pltpu.VMEM((3, 1, half), jnp.float32),
                pltpu.VMEM((3, 1, half), jnp.float32),
                dma,
                dma((3,)), dma((3,)), dma((3,)),
                dma((4,)), dma((2,)), dma((2,)),
                dma((3, 2)), dma((3, 2)),
                dma((width,)), dma((width,)), dma((width,)),
            ],
            compiler_params=pltpu.CompilerParams(
                collective_id=0, has_side_effects=True, vmem_limit_bytes=62 * 1024 * 1024
            ),
            cost_estimate=pl.CostEstimate(flops=flops, bytes_accessed=40_000_000, transcendentals=0),
        )(
            jnp.swapaxes(images, 1, 2),
            w_conv1.reshape(9, ch, half), b_conv1.reshape(1, half),
            w_conv2.reshape(9, half, ch), b_conv2.reshape(1, ch),
            w_conv3.reshape(9, ch, half), b_conv3.reshape(1, half),
        )
        return jnp.swapaxes(y, 1, 2)

    in_specs = (
        P("data", "spatial", None, None),
        P(None, None, None, "model"),
        P("model"),
        P(None, None, "model", None),
        P(None),
        P(None, None, None, "model"),
        P("model"),
    )
    return jax.shard_map(local_stack, mesh=mesh, in_specs=in_specs, out_specs=P("data", "spatial", None, "model"), check_vma=False)
```

time: 210 us -> 76.1 us (0.36)
  the two profiles are of different devices: /device:TPU:30 before, /device:TPU:1 now
where the time goes in v1:
time: 76.1 us; the launch traced here: 75.9 us
  Pallas kernels  71.8 us (94%)
  local copies, waits for them, and re-layouts  4.13 us (5%)
    pallas_call x1, Pallas kernels, local_stack(): pl.pallas_call(functools.partial(kernel, (n_band, batch, height, width, c...  71.8 us
    unnamed x1, local copies, waits for them, and re-layouts  4.13 us

profile of v1, /device:TPU:1, one launch (start us, length us, event | category | flops | bytes accessed | tf_op | source)
XLA Modules:
  0.0 75.9 jit_solution(1162021432464941284)
XLA Ops:
  0.0 71.8 %shard_map.73 = bf16[32,14,16,256]{3,2,1,0:T(8,128)(2,1)} custom-call(bf16[32,14,16,512]{3,2,1,0:T(8,128)(2,1)} %bitcast.9, bf16[9,512,256]{2,1,0:T(8,128)(2,1)} %bitcast.10, f32[1,256]{1,0:T(1,128)} %bitcast.14, bf16[9,256,512]{2,1,0:T(8,128)(2,1)} %bitcast.11, f32[1,512]{1,0:T(1,128)} %bitcast.13, bf16[9,512,256]{2,1,0:T(8,128)(2,1)} %bitcast.12, ...), custom_call_target="tpu_custom_call" | custom-call | flops 50734301184 | bytes 40000000 | tf_op jit(solution)/shard_map/pallas_call | solution.py:203
  71.8 4.1 %copy.9 = bf16[32,16,14,256]{3,1,2,0:T(8,128)(2,1)} copy(bf16[32,16,14,256]{3,1,2,0:T(8,128)(2,1)} %bitcast.8) | data formatting | bytes 7340032

commit v2 on v0

v2 whole, which is shorter than its diff:
```python
import functools

import jax
import jax.numpy as jnp
from jax import lax
from jax.experimental import pallas as pl
from jax.experimental.pallas import tpu as pltpu
from jax.sharding import PartitionSpec as P

MESH = pl.DeviceIdType.MESH
ROWS = 4
VMEM_LIMIT = 48 * 1024 * 1024


def convs(
    dims, img, w1, b1, w2, b2, w3, b3, own, far,
    stage, act, wts, bias_own, bias_far,
    img_sem, w_sem, w_send, w_recv, b_sem, b_send, b_recv, h_send, h_recv, o_send, o_recv,
):
    n_band, per_core, height, width, ch = dims
    half = ch // 2
    core = lax.axis_index("model")
    band = lax.axis_index("spatial")
    data = lax.axis_index("data")
    first, final = band == 0, band == n_band - 1
    above, below = jnp.maximum(band - 1, 0), jnp.minimum(band + 1, n_band - 1)
    sibling = (data, band, 1 - core)

    def image_in(col):
        return pltpu.make_async_copy(img.at[pl.ds(core * per_core, per_core), col], stage.at[:, col], img_sem.at[col])

    own_parts = [wts.at[0, :, :, 0:half], wts.at[1, :, 0:half, :], wts.at[2, :, :, 0:half]]
    far_parts = [wts.at[0, :, :, half:ch], wts.at[1, :, half:ch, :], wts.at[2, :, :, half:ch]]
    w_in = [pltpu.make_async_copy(w, own_parts[i], w_sem.at[i]) for i, w in enumerate((w1, w2, w3))]
    w_far = [
        pltpu.make_async_remote_copy(w, far_parts[i], w_send.at[i], w_recv.at[i], device_id=sibling, device_id_type=MESH)
        for i, w in enumerate((w1, w2, w3))
    ]
    b_in = [
        pltpu.make_async_copy(b1, bias_own.at[0], b_sem.at[0]),
        pltpu.make_async_copy(b2.at[:, 0:half], bias_own.at[1], b_sem.at[1]),
        pltpu.make_async_copy(b2.at[:, half:ch], bias_far.at[1], b_sem.at[2]),
        pltpu.make_async_copy(b3, bias_own.at[2], b_sem.at[3]),
    ]
    b_far = [
        pltpu.make_async_remote_copy(b, bias_far.at[i], b_send.at[k], b_recv.at[k], device_id=sibling, device_id_type=MESH)
        for k, (b, i) in enumerate(((b1, 0), (b3, 2)))
    ]

    barrier = pltpu.get_barrier_semaphore()
    pl.semaphore_signal(barrier, inc=1, device_id=sibling, device_id_type=MESH)

    @pl.when(jnp.logical_not(first))
    def _():
        pl.semaphore_signal(barrier, inc=1, device_id=(data, above, core), device_id_type=MESH)

    @pl.when(jnp.logical_not(final))
    def _():
        pl.semaphore_signal(barrier, inc=1, device_id=(data, below, core), device_id_type=MESH)

    for col in range(width):
        image_in(col).start()
    w_in[0].start()
    for c in b_in:
        c.start()
    pl.semaphore_wait(barrier, 3 - first.astype(jnp.int32) - final.astype(jnp.int32))
    w_far[0].start()
    for c in b_far:
        c.start()

    zero_row = jnp.zeros((width, per_core, ch), jnp.bfloat16)
    zero_col = jnp.zeros((1, per_core, ch), jnp.bfloat16)

    def zero(level, _):
        def cols(r, _):
            act[level, r, 0:1] = zero_col
            act[level, r, width + 1 : width + 2] = zero_col
            return 0

        lax.fori_loop(0, height + 2, cols, 0)

        @pl.when(first)
        def _():
            act[level, 0, 1 : width + 1] = zero_row

        @pl.when(final)
        def _():
            act[level, height + 1, 1 : width + 1] = zero_row

        return 0

    lax.fori_loop(0, 3, zero, 0)

    def halo_up(level):
        return pltpu.make_async_remote_copy(
            act.at[level, 1, 1 : width + 1], act.at[level, height + 1, 1 : width + 1],
            h_send.at[level, 0], h_recv.at[level, 0], device_id=(data, above, core), device_id_type=MESH,
        )

    def halo_down(level):
        return pltpu.make_async_remote_copy(
            act.at[level, height, 1 : width + 1], act.at[level, 0, 1 : width + 1],
            h_send.at[level, 1], h_recv.at[level, 1], device_id=(data, below, core), device_id_type=MESH,
        )

    def send_halo(level):
        @pl.when(jnp.logical_not(first))
        def _():
            halo_up(level).start()

        @pl.when(jnp.logical_not(final))
        def _():
            halo_down(level).start()

    def wait_halo(level):
        @pl.when(jnp.logical_not(final))
        def _():
            halo_up(level).wait_recv()

        @pl.when(jnp.logical_not(first))
        def _():
            halo_down(level).wait_recv()

    def sent_halo(level):
        @pl.when(jnp.logical_not(first))
        def _():
            halo_up(level).wait_send()

        @pl.when(jnp.logical_not(final))
        def _():
            halo_down(level).wait_send()

    def take(col, _):
        image_in(col).wait()
        act[0, 1 : height + 1, col + 1] = jnp.swapaxes(stage[:, col], 0, 1)
        return 0

    lax.fori_loop(0, width, take, 0)
    send_halo(0)
    w_in[1].start()
    w_in[2].start()
    w_far[1].start()
    w_far[2].start()

    def conv(level, rows, lo, hi):
        m = width * per_core
        taps = []
        for dh in range(3):
            for dw in range(3):
                views = [act[level, r + dh, dw : dw + width].reshape(m, ch) for r in rows]
                taps.append(jnp.concatenate(views, axis=0))
        lhs = jnp.concatenate(taps, axis=1)
        total = jnp.dot(lhs, wts[level, :, :, lo:hi].reshape(9 * ch, hi - lo), preferred_element_type=jnp.float32)
        bias = ([bias_own[level]] if lo == 0 else []) + ([bias_far[level]] if hi == ch else [])
        total = total + (jnp.concatenate(bias, axis=1) if len(bias) > 1 else bias[0])
        return jnp.maximum(total, 0.0).astype(jnp.bfloat16).reshape(len(rows), width, per_core, hi - lo)

    def step(level, rows, lo=0, hi=ch):
        y = conv(level, rows, lo, hi)
        for i, r in enumerate(rows):
            act[level + 1, r + 1, 1 : width + 1, :, lo:hi] = y[i]

    inner = [list(range(r, min(r + ROWS, height - 1))) for r in range(1, height - 1, ROWS)]
    outer = [height - 1, 0]

    w_in[0].wait()
    for c in b_in:
        c.wait()
    for rows in inner[:2]:
        step(0, rows, 0, half)
    w_far[0].wait_recv()
    for c in b_far:
        c.wait_recv()
    for rows in inner[:2]:
        step(0, rows, half, ch)
    for rows in inner[2:]:
        step(0, rows)
    wait_halo(0)
    step(0, outer)
    send_halo(1)

    w_in[1].wait()
    w_far[1].wait_recv()
    for rows in inner:
        step(1, rows)
    wait_halo(1)
    step(1, outer)
    send_halo(2)

    def to_sibling(r):
        return pltpu.make_async_remote_copy(
            act.at[0, r + 1, 1 : width + 1, :, half:ch], far.at[r], o_send.at[r], o_recv.at[r],
            device_id=sibling, device_id_type=MESH,
        )

    w_in[2].wait()
    w_far[2].wait_recv()
    sent_halo(0)
    for rows in inner:
        y = conv(2, rows, 0, ch)
        for i, r in enumerate(rows):
            act[0, r + 1, 1 : width + 1, :, half:ch] = y[i, :, :, half:ch]
            own[r] = y[i, :, :, 0:half]
        for r in rows:
            to_sibling(r).start()
    wait_halo(2)
    y = conv(2, outer, half, ch)
    for i, r in enumerate(outer):
        act[0, r + 1, 1 : width + 1, :, half:ch] = y[i]
    for r in outer:
        to_sibling(r).start()
    y = conv(2, outer, 0, half)
    for i, r in enumerate(outer):
        own[r] = y[i]

    for i in range(3):
        w_far[i].wait_send()
    for level in (1, 2):
        sent_halo(level)
    for c in b_far:
        c.wait_send()
    for r in range(height):
        to_sibling(r).wait_send()
        to_sibling(r).wait_recv()


def write(dims, own, far, out, stage, sem):
    per_core, height, width, half = dims
    core = lax.axis_index("model")

    def put(k, col):
        image = jnp.where(k == 0, core, 1 - core) * per_core
        return pltpu.make_async_copy(stage.at[k, :, col], out.at[pl.ds(image, per_core), col], sem.at[k, col])

    def column(col, _):
        for k, part in enumerate((own, far)):
            stage[k, :, col] = jnp.swapaxes(part[:, col], 0, 1)
            put(k, col).start()
        return 0

    lax.fori_loop(0, width, column, 0)

    def finish(col, _):
        for k in range(2):
            put(k, col).wait()
        return 0

    lax.fori_loop(0, width, finish, 0)


def solution(mesh):
    n_band = mesh.shape["spatial"]

    def local_stack(images, w_conv1, b_conv1, w_conv2, b_conv2, w_conv3, b_conv3):
        batch, height, width, ch = images.shape
        half, per_core = ch // 2, batch // 2
        hbm = pl.BlockSpec(memory_space=pltpu.HBM)
        vmem = pl.BlockSpec(memory_space=pltpu.VMEM)
        dma = pltpu.SemaphoreType.DMA
        part = (height, width, per_core, half)
        args = (
            jnp.swapaxes(images, 1, 2),
            w_conv1.reshape(9, ch, half), b_conv1.reshape(1, half),
            w_conv2.reshape(9, half, ch), b_conv2.reshape(1, ch),
            w_conv3.reshape(9, ch, half), b_conv3.reshape(1, half),
        )
        own, far = pl.pallas_call(
            functools.partial(convs, (n_band, per_core, height, width, ch)),
            out_shape=[pltpu.VMEM(part, jnp.bfloat16)] * 2,
            in_specs=[hbm] * 7,
            out_specs=[vmem] * 2,
            scratch_shapes=[
                pltpu.VMEM((per_core, width, height, ch), jnp.bfloat16),
                pltpu.VMEM((3, height + 2, width + 2, per_core, ch), jnp.bfloat16),
                pltpu.VMEM((3, 9, ch, ch), jnp.bfloat16),
                pltpu.VMEM((3, 1, half), jnp.float32),
                pltpu.VMEM((3, 1, half), jnp.float32),
                dma((width,)),
                dma((3,)), dma((3,)), dma((3,)),
                dma((4,)), dma((2,)), dma((2,)),
                dma((3, 2)), dma((3, 2)),
                dma((height,)), dma((height,)),
            ],
            compiler_params=pltpu.CompilerParams(
                collective_id=0, has_side_effects=True, vmem_limit_bytes=VMEM_LIMIT
            ),
            cost_estimate=pl.CostEstimate(
                flops=2 * 3 * 9 * per_core * height * width * ch * ch, bytes_accessed=20_000_000, transcendentals=0
            ),
        )(*[pltpu.with_memory_space_constraint(a, pltpu.HBM) for a in args])
        y = pl.pallas_call(
            functools.partial(write, (per_core, height, width, half)),
            out_shape=jax.ShapeDtypeStruct((batch, width, height, half), jnp.bfloat16),
            in_specs=[vmem] * 2,
            out_specs=hbm,
            scratch_shapes=[pltpu.VMEM((2, per_core, width, height, half), jnp.bfloat16), dma((2, width))],
            compiler_params=pltpu.CompilerParams(vmem_limit_bytes=16 * 1024 * 1024),
        )(own, far)
        return jnp.swapaxes(y, 1, 2)

    in_specs = (
        P("data", "spatial", None, None),
        P(None, None, None, "model"),
        P("model"),
        P(None, None, "model", None),
        P(None),
        P(None, None, None, "model"),
        P("model"),
    )
    return jax.shard_map(local_stack, mesh=mesh, in_specs=in_specs, out_specs=P("data", "spatial", None, "model"), check_vma=False)
```

time: 210 us -> 64.6 us (0.31)
  the two profiles are of different devices: /device:TPU:30 before, /device:TPU:96 now
where the time goes in v2:
time: 64.6 us; the launch traced here: 64.5 us
  Pallas kernels  64.3 us (100%)
    pallas_call x1, Pallas kernels, local_stack(): pl.pallas_call(functools.partial(convs, (n_band, per_core, height, width,...  62.2 us
    pallas_call x1, Pallas kernels, local_stack(): pl.pallas_call(functools.partial(write, (per_core, height, width, half)),...  2.1 us

profile of v2, /device:TPU:96, one launch (start us, length us, event | category | flops | bytes accessed | tf_op | source)
XLA Modules:
  0.0 64.5 jit_solution(12931211117726942920)
XLA Ops:
  0.0 62.2 %shard_map.73 = (bf16[16,14,16,256]{3,2,1,0:T(8,128)(2,1)S(1)}, bf16[16,14,16,256]{3,2,1,0:T(8,128)(2,1)S(1)}) custom-call(bf16[32,14,16,512]{3,2,1,0:T(8,128)(2,1)} %bitcast.8, bf16[9,512,256]{2,1,0:T(8,128)(2,1)} %bitcast.9, f32[1,256]{1,0:T(1,128)} %bitcast.13, bf16[9,256,512]{2,1,0:T(8,128)(2,1)} %bitcast.10, f32[1,512]{1,0:T(1,128)} %bitcast.12, ...), custom_call_target="tpu_custom_call" | custom-call | flops 50734301184 | bytes 20000000 | tf_op jit(solution)/shard_map/pallas_call | solution.py:267
  62.2 2.1 %shard_map.74 = bf16[32,14,16,256]{3,2,1,0:T(8,128)(2,1)} custom-call(bf16[16,14,16,256]{3,2,1,0:T(8,128)(2,1)S(1)} %get-tuple-element.7.own, bf16[16,14,16,256]{3,2,1,0:T(8,128)(2,1)S(1)} %get-tuple-element.8.far), custom_call_target="tpu_custom_call" | custom-call | tf_op jit(solution)/shard_map/pallas_call | solution.py:291

commit v3 on v2

--- a/solution.py
+++ b/solution.py
@@ -9,6 +9,7 @@
 
 MESH = pl.DeviceIdType.MESH
 ROWS = 4
+LINE = 4
 VMEM_LIMIT = 48 * 1024 * 1024
 
 
@@ -103,12 +104,18 @@
             h_send.at[level, 1], h_recv.at[level, 1], device_id=(data, below, core), device_id_type=MESH,
         )
 
+    line_end = lax.rem(band, LINE) == LINE - 1
+
     def send_halo(level):
+        @pl.when(jnp.logical_and(line_end, jnp.logical_not(final)))
+        def _():
+            halo_down(level).start()
+
         @pl.when(jnp.logical_not(first))
         def _():
             halo_up(level).start()
 
-        @pl.when(jnp.logical_not(final))
+        @pl.when(jnp.logical_not(jnp.logical_or(line_end, final)))
         def _():
             halo_down(level).start()
 
@@ -196,22 +203,31 @@
     w_in[2].wait()
     w_far[2].wait_recv()
     sent_halo(0)
-    for rows in inner:
-        y = conv(2, rows, 0, ch)
+    def last(rows, lo, hi):
+        y = conv(2, rows, lo, hi)
         for i, r in enumerate(rows):
-            act[0, r + 1, 1 : width + 1, :, half:ch] = y[i, :, :, half:ch]
-            own[r] = y[i, :, :, 0:half]
-        for r in rows:
-            to_sibling(r).start()
+            if lo == 0:
+                own[r] = y[i, :, :, 0:half]
+            if hi == ch:
+                act[0, r + 1, 1 : width + 1, :, half:ch] = y[i, :, :, half - lo : ch - lo]
+
+    def send(groups):
+        for rows in groups:
+            for r in rows:
+                to_sibling(r).start()
+
+    for rows in inner[:2]:
+        last(rows, 0, ch)
+    send(inner[:2])
+    for rows in inner[2:]:
+        last(rows, 0, ch)
+    send(inner[2:])
     wait_halo(2)
-    y = conv(2, outer, half, ch)
-    for i, r in enumerate(outer):
-        act[0, r + 1, 1 : width + 1, :, half:ch] = y[i]
     for r in outer:
-        to_sibling(r).start()
-    y = conv(2, outer, 0, half)
-    for i, r in enumerate(outer):
-        own[r] = y[i]
+        last([r], half, ch)
+    send([outer])
+    for r in outer:
+        last([r], 0, half)
 
     for i in range(3):
         w_far[i].wait_send()

time: 64.6 us -> 62.6 us (0.969)
  the two profiles are of different devices: /device:TPU:96 before, /device:TPU:97 now
where the time goes in v3:
time: 62.6 us; the launch traced here: 62.5 us
  Pallas kernels  62.3 us (100%)
    pallas_call x1, Pallas kernels, local_stack(): pl.pallas_call(functools.partial(convs, (n_band, per_core, height, width,...  60.2 us
    pallas_call x1, Pallas kernels, local_stack(): pl.pallas_call(functools.partial(write, (per_core, height, width, half)),...  2.1 us

profile of v3, /device:TPU:97, one launch (start us, length us, event | category | flops | bytes accessed | tf_op | source)
XLA Modules:
  0.0 62.5 jit_solution(8299676015049734856)
XLA Ops:
  0.0 60.2 %shard_map.73 = (bf16[16,14,16,256]{3,2,1,0:T(8,128)(2,1)S(1)}, bf16[16,14,16,256]{3,2,1,0:T(8,128)(2,1)S(1)}) custom-call(bf16[32,14,16,512]{3,2,1,0:T(8,128)(2,1)} %bitcast.8, bf16[9,512,256]{2,1,0:T(8,128)(2,1)} %bitcast.9, f32[1,256]{1,0:T(1,128)} %bitcast.13, bf16[9,256,512]{2,1,0:T(8,128)(2,1)} %bitcast.10, f32[1,512]{1,0:T(1,128)} %bitcast.12, ...), custom_call_target="tpu_custom_call" | custom-call | flops 50734301184 | bytes 20000000 | tf_op jit(solution)/shard_map/pallas_call | solution.py:283
  60.2 2.1 %shard_map.74 = bf16[32,14,16,256]{3,2,1,0:T(8,128)(2,1)} custom-call(bf16[16,14,16,256]{3,2,1,0:T(8,128)(2,1)S(1)} %get-tuple-element.7.own, bf16[16,14,16,256]{3,2,1,0:T(8,128)(2,1)S(1)} %get-tuple-element.8.far), custom_call_target="tpu_custom_call" | custom-call | tf_op jit(solution)/shard_map/pallas_call | solution.py:307

commit v4 on v3

--- a/solution.py
+++ b/solution.py
@@ -64,10 +64,6 @@
     w_in[0].start()
     for c in b_in:
         c.start()
-    pl.semaphore_wait(barrier, 3 - first.astype(jnp.int32) - final.astype(jnp.int32))
-    w_far[0].start()
-    for c in b_far:
-        c.start()
 
     zero_row = jnp.zeros((width, per_core, ch), jnp.bfloat16)
     zero_col = jnp.zeros((1, per_core, ch), jnp.bfloat16)
@@ -143,11 +139,8 @@
         return 0
 
     lax.fori_loop(0, width, take, 0)
-    send_halo(0)
     w_in[1].start()
     w_in[2].start()
-    w_far[1].start()
-    w_far[2].start()
 
     def conv(level, rows, lo, hi):
         m = width * per_core
@@ -173,15 +166,24 @@
     w_in[0].wait()
     for c in b_in:
         c.wait()
-    for rows in inner[:2]:
+    step(0, [1, 2], 0, half)
+    step(0, [3, 4], 0, half)
+    pl.semaphore_wait(barrier, 3 - first.astype(jnp.int32) - final.astype(jnp.int32))
+    w_far[0].start()
+    for c in b_far:
+        c.start()
+    send_halo(0)
+    w_far[1].start()
+    w_far[2].start()
+    rest = list(range(5, height - 1))
+    pairs = [rest[:4], rest[4:8]] + [[r] for r in rest[8:]]
+    for rows in pairs:
         step(0, rows, 0, half)
     w_far[0].wait_recv()
     for c in b_far:
         c.wait_recv()
-    for rows in inner[:2]:
+    for rows in ([1, 2, 3, 4], rest[:4], rest[4:7], rest[7:]):
         step(0, rows, half, ch)
-    for rows in inner[2:]:
-        step(0, rows)
     wait_halo(0)
     step(0, outer)
     send_halo(1)

time: 62.6 us -> 59.9 us (0.957)
  the two profiles are of different devices: /device:TPU:97 before, /device:TPU:1 now
where the time goes in v4:
time: 59.9 us; the launch traced here: 59.8 us
  Pallas kernels  59.7 us (100%)
    pallas_call x1, Pallas kernels, local_stack(): pl.pallas_call(functools.partial(convs, (n_band, per_core, height, width,...  57.6 us
    pallas_call x1, Pallas kernels, local_stack(): pl.pallas_call(functools.partial(write, (per_core, height, width, half)),...  2.1 us

profile of v4, /device:TPU:1, one launch (start us, length us, event | category | flops | bytes accessed | tf_op | source)
XLA Modules:
  0.0 59.8 jit_solution(10951521115253815353)
XLA Ops:
  0.0 57.6 %shard_map.73 = (bf16[16,14,16,256]{3,2,1,0:T(8,128)(2,1)S(1)}, bf16[16,14,16,256]{3,2,1,0:T(8,128)(2,1)S(1)}) custom-call(bf16[32,14,16,512]{3,2,1,0:T(8,128)(2,1)} %bitcast.8, bf16[9,512,256]{2,1,0:T(8,128)(2,1)} %bitcast.9, f32[1,256]{1,0:T(1,128)} %bitcast.13, bf16[9,256,512]{2,1,0:T(8,128)(2,1)} %bitcast.10, f32[1,512]{1,0:T(1,128)} %bitcast.12, ...), custom_call_target="tpu_custom_call" | custom-call | flops 50734301184 | bytes 20000000 | tf_op jit(solution)/shard_map/pallas_call | solution.py:285
  57.6 2.1 %shard_map.74 = bf16[32,14,16,256]{3,2,1,0:T(8,128)(2,1)} custom-call(bf16[16,14,16,256]{3,2,1,0:T(8,128)(2,1)S(1)} %get-tuple-element.7.own, bf16[16,14,16,256]{3,2,1,0:T(8,128)(2,1)S(1)} %get-tuple-element.8.far), custom_call_target="tpu_custom_call" | custom-call | tf_op jit(solution)/shard_map/pallas_call | solution.py:309
